TPU v7x, 32 devices: a whole 2x2x4 slice. The times are simulated.
32 devices in a mesh: wide: 8 (over y, x, core), narrow: 4 (over z).
Axes of the slice: x: 2, y: 2, z: 4, core: 2. Of those that a mesh axis runs over, the one named last changes fastest.
Arguments:
- coefficients: float32 [8, 8192, 8192], P(None, 'wide', 'narrow'), may hold values from -0.07 to 0.07
- tensor_blocks: float32 [8, 32, 8192], P(None, 'wide', 'narrow'), may hold values from -6 to 6
- basis_rows: float32 [32, 8192], P(None, ('wide', 'narrow')), may hold values from -1.1 to 1.1, as said below
Outputs:
- new_basis: float32 [32, 8192], P(None, ('wide', 'narrow'))
- projection: float32 [32, 32], replicated
- factor: float32 [32, 32], replicated
Inputs may be any that keep to these rules, and one draw needn't show every extreme that they name: The rows of basis_rows are nearly but not exactly orthonormal: basis_rows basis_rows^T differs from the identity by less than 0.2 in spectral norm.
All inputs are finite; a program needn't handle non-finite values.
Results may differ from a plain program's by a relative error of at most 0.0002.
Values sent between devices are 32-bit elements; how exact they have to be, the bound alone decides.
A program may use at most 128 MiB of HBM per device.

v0:
```python
import jax
import jax.numpy as jnp
from jax import lax
from jax.sharding import PartitionSpec as P

N = 8192


def body(coefficients, tensor_blocks, basis_rows):
    hi = lax.Precision.HIGHEST
    partial_block = jnp.einsum(
        "kic,krc->ir",
        lax.all_gather(tensor_blocks, "wide", axis=1, tiled=True),
        coefficients,
        precision=hi,
    )
    image = lax.psum_scatter(partial_block, "narrow", scatter_dimension=1, tiled=True)
    local_first = jnp.dot(basis_rows, image.T, precision=hi)
    local_correlation = jnp.dot(basis_rows, basis_rows.T, precision=hi)
    first, correlation = lax.psum((local_first, local_correlation), ("wide", "narrow"))
    once = image - jnp.dot(first.T, basis_rows, precision=hi)
    second, raw_gram = lax.psum(
        (jnp.dot(basis_rows, once.T, precision=hi), jnp.dot(once, once.T, precision=hi)),
        ("wide", "narrow"),
    )
    twice = once - jnp.dot(second.T, basis_rows, precision=hi)
    cross = jnp.dot(second.T, second, precision=hi)
    weighted = jnp.dot(second.T, jnp.dot(correlation, second, precision=hi), precision=hi)
    gram = (raw_gram - 2.0 * cross + weighted) / N
    factor = jnp.linalg.cholesky(gram)
    new_basis = lax.linalg.triangular_solve(factor, twice, left_side=True, lower=True)
    return (new_basis, first + second, factor)


def solution(mesh):
    in_specs = (P(None, "wide", "narrow"), P(None, "wide", "narrow"), P(None, ("wide", "narrow")))
    out_specs = (P(None, ("wide", "narrow")), P(), P())
    return jax.shard_map(body, mesh=mesh, in_specs=in_specs, out_specs=out_specs, check_vma=False)
```

profile of v0, /device:TPU:0, one launch (start us, length us, event | category | flops | bytes accessed | tf_op | source)
XLA Modules:
  0.0 225.5 jit_solution(1987830653347588551)
XLA Ops:
  7.2 0.0 copy-start
  7.2 0.0 all-gather.2.cloned.1.call-start
  7.2 1.8 copy.11
  9.1 0.0 all-gather.2.cloned.1.call-update
  9.1 0.0 reduce-scatter.2.cloned.1.call-start
  9.1 31.3 %all-gather.2.cloned.1.call-done = f32[8,32,2048]{2,0,1:T(8,128)} async-done(((f32[8,4,2048]{2,0,1:T(8,128)}), f32[8,32,2048]{2,0,1:T(8,128)}) %all-gather.2.cloned.1.call-update) | async-done | bytes 2097168 | tf_op jit(solution)/shard_map/all_gather | solution.py:13
  40.4 67.1 %fusion.2 = f32[32,1024]{1,0:T(8,128)} fusion(f32[8,1024,2048]{2,1,0:T(8,128)} %param.3, f32[8,32,2048]{2,0,1:T(8,128)} %all-gather.2.cloned.1.call-done), kind=kOutput, calls=%fused_computation.2 | convolution fusion | flops 6442450944 | bytes 69337088 | tf_op jit(solution)/shard_map/kic,krc->ir/dot_general | solution.py:11
  107.5 0.0 reduce-scatter.2.cloned.1.call-update
  107.5 0.0 copy-done
  107.5 0.2 fusion.11
  107.7 19.4 %reduce-scatter.2.cloned.1.call-done = f32[32,256]{1,0:T(8,128)} async-done(((f32[32,1024]{1,0:T(8,128)}), f32[32,256]{1,0:T(8,128)}) %reduce-scatter.2.cloned.1.call-update) | async-done | bytes 32784 | tf_op jit(solution)/shard_map/reduce_scatter | solution.py:17
  127.1 0.9 convolution_bitcast_fusion.1
  128.1 38.5 %psum.28 = f32[32,32]{0,1:T(8,128)S(1)} all-reduce(f32[32,32]{0,1:T(8,128)S(1)} %convolution_bitcast_fusion.1), channel_id=1, replica_groups=mesh['wide'=8,'narrow'=4] {'wide','narrow'}, use_global_device_ids=true, to_apply=%region_1.0 | all-reduce | flops 1024 | bytes 8192 | tf_op jit(solution)/shard_map/psum | solution.py:20
  166.5 0.9 convolution_subtract_fusion.1
  167.4 0.2 convolution_bitcast_fusion
  167.6 0.2 fusion.10
  167.8 41.3 %all-reduce = (f32[32,32]{0,1:T(8,128)S(1)}, f32[32,32]{0,1:T(8,128)S(1)}, f32[32,32]{1,0:T(8,128)S(1)}) all-reduce(f32[32,32]{0,1:T(8,128)S(1)} %convolution_bitcast_fusion, f32[32,32]{0,1:T(8,128)S(1)} %fusion.10, f32[32,32]{1,0:T(8,128)S(1)} %fusion.11), channel_id=1, replica_groups=mesh['wide'=8,'narrow'=4] {'wide','narrow'}, use_global_device_ids=true, to_apply=%region_3.0 | all-reduce | flops 3072 | bytes 24576 | tf_op jit(solution)/shard_map/psum | solution.py:22
  209.1 0.2 convolution_subtract_fusion
  209.2 0.1 fusion.12
  209.4 0.2 fusion.6
  209.6 0.2 fusion.5
  209.8 0.1 copy.16
  209.9 2.9 %cholesky.16 = f32[32,32]{1,0:T(8,128)S(1)} custom-call(f32[32,32]{1,0:T(8,128)S(1)} %fusion.9), custom_call_target="Cholesky" | custom-call | tf_op jit(solution)/shard_map/jit(cholesky)/cholesky | solution.py:30
  212.8 0.6 compare_reduce_fusion
  213.5 1.3 select_bitcast_fusion
  214.7 2.4 %custom-call.6 = f32[1,32,32]{1,2,0:T(8,128)S(1)} custom-call(f32[1,32,32]{2,1,0:T(8,128)S(1)} %get-tuple-element.12), custom_call_target="InvertDiagBlocksLowerTriangular" | custom-call | tf_op jit(solution)/shard_map/triangular_solve | solution.py:31
  217.1 0.7 copy.17
  217.9 0.8 fusion.7
  (3 shorter events, 0.0 us)
Async XLA Ops:
  7.2 100.4 %copy-start = (f32[32,256]{1,0:T(8,128)S(1)}, f32[32,256]{1,0:T(8,128)}, u32[]{:S(2)}) copy-start(f32[32,256]{1,0:T(8,128)} %param.5) | copy-start | bytes 98308
  7.2 33.2 %all-gather.2.cloned.1.call-start = ((), (), s32[]{:S(2)}) async-start(), calls=%async_computation.1 | async-start | bytes 2359296 | tf_op jit(solution)/shard_map/all_gather | solution.py:13
  9.1 118.1 %reduce-scatter.2.cloned.1.call-start = ((), (), s32[]{:S(2)}) async-start(), calls=%async_computation.2 | async-start | bytes 163840 | tf_op jit(solution)/shard_map/reduce_scatter | solution.py:17
Sparse Core Ops, SparseCore 0:
  9.9 30.4 all-gather.1
  107.7 19.4 reduce-scatter.1
where the time goes:
time: 226 us
  blocking collectives  79.7 us (35%)
  matrix products  70.9 us (31%)
  waiting for transfers between devices  50.7 us (22%)
  between operations  14.1 us (6%)
  other arithmetic  7.3 us (3%)
  local copies, waits for them, and re-layouts  2.62 us (1%)
    dot_general x1, matrix products, body(): jnp.einsum('kic,krc->ir', lax.all_gather(tensor_blocks, 'wide', axis=1, t...  67.1 us
    psum x1, blocking collectives, body(): lax.psum((jnp.dot(basis_rows, once.T, precision=hi), jnp.dot(once, once.T...  41.3 us
    psum x1, blocking collectives, body(): lax.psum((local_first, local_correlation), ('wide', 'narrow'))  38.5 us
    all_gather x1, waiting for transfers between devices, body(): lax.all_gather(tensor_blocks, 'wide', axis=1, tiled=True)  31.3 us
    reduce_scatter x1, waiting for transfers between devices, body(): lax.psum_scatter(partial_block, 'narrow', scatter_dimension=1, tiled=True)  19.4 us
  transfers between devices with their start and end apart: 2, of which 2 were waited for; matrix products, arithmetic and copies ran while one was open for 0% of the time, Pallas kernels for 0%

commit v1 on v0

--- a/solution.py
+++ b/solution.py
@@ -1,3 +1,4 @@
+import functools
 import jax
 import jax.numpy as jnp
 from jax import lax
@@ -6,13 +7,28 @@
 N = 8192
 
 
+def resolve_waves(chunk, axis_id):
+    tall = jax.lax.axis_index(axis_id)
+    carry_in = jax.lax.axis_size(axis_id)
+    carry, response = (carry_in, tall)
+    then, near = (chunk, 1)
+    while near < carry:
+        local_now = tuple(((src_i, src_i ^ near) for src_i in range(carry)))
+        fresh = jax.lax.ppermute(then, axis_id, local_now)
+        q_next = jnp.concatenate([then, fresh], axis=1)
+        o_now = jnp.concatenate([fresh, then], axis=1)
+        then = jnp.where(response & near == 0, q_next, o_now)
+        near = 2 * near
+    return then
+
+
+form_digits = functools.partial(resolve_waves, axis_id="wide")
+
+
 def body(coefficients, tensor_blocks, basis_rows):
     hi = lax.Precision.HIGHEST
     partial_block = jnp.einsum(
-        "kic,krc->ir",
-        lax.all_gather(tensor_blocks, "wide", axis=1, tiled=True),
-        coefficients,
-        precision=hi,
+        "kic,krc->ir", form_digits(tensor_blocks), coefficients, precision=hi
     )
     image = lax.psum_scatter(partial_block, "narrow", scatter_dimension=1, tiled=True)
     local_first = jnp.dot(basis_rows, image.T, precision=hi)

time: 226 us -> 236 us (1.044)
  waiting for transfers between devices: 50.7 us -> 57.1 us
  starting transfers between devices: 0.08 us -> 5.34 us
    ppermute x0 -> x3, waiting for transfers between devices: none -> 36.5 us  [resolve_waves(): fresh = jax.lax.ppermute(then, axis_id, local_now)]
    all_gather x1 -> x0, waiting for transfers between devices: 31.3 us -> none  [body(): lax.all_gather(tensor_blocks, 'wide', axis=1, tiled=True)]
    ppermute x0 -> x3, starting transfers between devices: none -> 5.3 us  [resolve_waves(): fresh = jax.lax.ppermute(then, axis_id, local_now)]
  transfers between devices with their start and end apart: 2 -> 4, of which waited for: 2 -> 4; matrix products, arithmetic and copies ran while one was open for 0% -> 0% of each run, Pallas kernels for 0% -> 0%
where the time goes in v1:
time: 236 us; the launch traced here: 235 us
  blocking collectives  79.9 us (34%)
  matrix products  69.2 us (29%)
  waiting for transfers between devices  57.1 us (24%)
  between operations  14.1 us (6%)
  other arithmetic  8.62 us (4%)
  starting transfers between devices  5.34 us (2%)
    dot_general x1, matrix products, body(): jnp.einsum('kic,krc->ir', form_digits(tensor_blocks), coefficients, preci...  65.4 us
    psum x1, blocking collectives, body(): lax.psum((jnp.dot(basis_rows, once.T, precision=hi), jnp.dot(once, once.T...  41.4 us
    psum x1, blocking collectives, body(): lax.psum((local_first, local_correlation), ('wide', 'narrow'))  38.5 us
    ppermute x3, waiting for transfers between devices, resolve_waves(): fresh = jax.lax.ppermute(then, axis_id, local_now)  36.5 us
    reduce_scatter x1, waiting for transfers between devices, body(): lax.psum_scatter(partial_block, 'narrow', scatter_dimension=1, tiled=True)  20.6 us
    ppermute x3, starting transfers between devices, resolve_waves(): fresh = jax.lax.ppermute(then, axis_id, local_now)  5.3 us
  transfers between devices with their start and end apart: 4, of which 4 were waited for; matrix products, arithmetic and copies ran while one was open for 0% of the time, Pallas kernels for 0%

profile of v1, /device:TPU:0, one launch (start us, length us, event | category | flops | bytes accessed | tf_op | source)
XLA Modules:
  0.0 235.0 jit_solution(1899170188064316248)
XLA Ops:
  7.2 0.0 copy-start
  7.2 0.0 reduce-scatter.2.cloned.1.call-start
  7.2 0.6 collective-permute-start
  7.8 1.4 collective-permute-done
  9.2 1.2 maximum_select_fusion.5
  10.4 2.9 %collective-permute-start.1 = (f32[8,8,2048]{2,1,0:T(8,128)S(1)}, f32[8,8,2048]{2,1,0:T(8,128)S(1)}, u32[]{:S(2)}, u32[]{:S(2)}) collective-permute-start(f32[8,8,2048]{2,1,0:T(8,128)S(1)} %maximum_select_fusion.5), channel_id=1, source_target_pairs={{0,8},{4,12},{8,0},{12,4},{16,24},{20,28},{24,16},{28,20},{1,9},{5... | collective-permute-start | bytes 1572872 | tf_op jit(solution)/shard_map/ppermute | solution.py:17
  13.3 12.2 %collective-permute-done.1 = f32[8,8,2048]{2,1,0:T(8,128)S(1)} collective-permute-done((f32[8,8,2048]{2,1,0:T(8,128)S(1)}, f32[8,8,2048]{2,1,0:T(8,128)S(1)}, u32[]{:S(2)}, u32[]{:S(2)}) %collective-permute-start.1) | collective-permute-done | bytes 524320 | tf_op jit(solution)/shard_map/ppermute | solution.py:17
  25.5 0.1 maximum_select_fusion.4
  25.6 1.8 collective-permute-start.2
  27.5 22.9 %collective-permute-done.2 = f32[8,16,2048]{2,1,0:T(8,128)S(1)} collective-permute-done((f32[8,16,2048]{2,1,0:T(8,128)S(1)}, f32[8,16,2048]{2,1,0:T(8,128)S(1)}, u32[]{:S(2)}, u32[]{:S(2)}) %collective-permute-start.2) | collective-permute-done | bytes 1048608 | tf_op jit(solution)/shard_map/ppermute | solution.py:17
  50.3 65.4 %fusion.6 = f32[32,1024]{1,0:T(8,128)} fusion(f32[8,1024,2048]{2,1,0:T(8,128)} %param.3, f32[8,16,2048]{2,1,0:T(8,128)S(1)} %collective-permute-done.2, f32[8,16,2048]{2,1,0:T(8,128)S(1)} %maximum_select_fusion.4, pred[]{:T(512)S(6)} %eq.9), kind=kOutput, calls=%fused_computation.7 | convolution fusion | flops 6444023808 | bytes 69337088 | tf_op jit(solution)/shard_map/kic,krc->ir/dot_general | solution.py:30
  115.7 0.0 reduce-scatter.2.cloned.1.call-update
  115.7 0.0 copy-done
  115.7 0.2 fusion.15
  115.9 20.6 %reduce-scatter.2.cloned.1.call-done = f32[32,256]{1,0:T(8,128)} async-done(((f32[32,1024]{1,0:T(8,128)}), f32[32,256]{1,0:T(8,128)}) %reduce-scatter.2.cloned.1.call-update) | async-done | bytes 32784 | tf_op jit(solution)/shard_map/reduce_scatter | solution.py:33
  136.5 0.9 convolution_bitcast_fusion.1
  137.5 38.5 %psum.28 = f32[32,32]{0,1:T(8,128)S(1)} all-reduce(f32[32,32]{0,1:T(8,128)S(1)} %convolution_bitcast_fusion.1), channel_id=1, replica_groups=mesh['wide'=8,'narrow'=4] {'wide','narrow'}, use_global_device_ids=true, to_apply=%region_1.2 | all-reduce | flops 1024 | bytes 8192 | tf_op jit(solution)/shard_map/psum | solution.py:36
  175.9 0.9 convolution_subtract_fusion.1
  176.9 0.2 convolution_bitcast_fusion
  177.0 0.2 fusion.14
  177.2 41.4 %all-reduce = (f32[32,32]{0,1:T(8,128)S(1)}, f32[32,32]{0,1:T(8,128)S(1)}, f32[32,32]{1,0:T(8,128)S(1)}) all-reduce(f32[32,32]{0,1:T(8,128)S(1)} %convolution_bitcast_fusion, f32[32,32]{0,1:T(8,128)S(1)} %fusion.14, f32[32,32]{1,0:T(8,128)S(1)} %fusion.15), channel_id=1, replica_groups=mesh['wide'=8,'narrow'=4] {'wide','narrow'}, use_global_device_ids=true, to_apply=%region_3.4 | all-reduce | flops 3072 | bytes 24576 | tf_op jit(solution)/shard_map/psum | solution.py:38
  218.6 0.2 convolution_subtract_fusion
  218.7 0.7 copy.10
  219.4 0.1 fusion.16
  219.6 0.2 fusion.8
  219.7 0.2 fusion.7
  220.0 0.1 copy.9
  220.0 2.9 %cholesky.16 = f32[32,32]{1,0:T(8,128)S(1)} custom-call(f32[32,32]{1,0:T(8,128)S(1)} %fusion.12), custom_call_target="Cholesky" | custom-call | tf_op jit(solution)/shard_map/jit(cholesky)/cholesky | solution.py:46
  223.0 0.6 compare_reduce_fusion
  223.6 1.3 select_bitcast_fusion
  224.9 2.4 %custom-call.6 = f32[1,32,32]{1,2,0:T(8,128)S(1)} custom-call(f32[1,32,32]{2,1,0:T(8,128)S(1)} %get-tuple-element.9), custom_call_target="InvertDiagBlocksLowerTriangular" | custom-call | tf_op jit(solution)/shard_map/triangular_solve | solution.py:47
  227.3 0.9 fusion.10
  (3 shorter events, 0.0 us)
Async XLA Ops:
  7.2 108.6 %copy-start = (f32[32,256]{1,0:T(8,128)S(1)}, f32[32,256]{1,0:T(8,128)}, u32[]{:S(2)}) copy-start(f32[32,256]{1,0:T(8,128)} %param.5) | copy-start | bytes 98308
  7.2 129.3 %reduce-scatter.2.cloned.1.call-start = ((), (), s32[]{:S(2)}) async-start(), calls=%async_computation.1 | async-start | bytes 163840 | tf_op jit(solution)/shard_map/reduce_scatter | solution.py:33
  7.2 1.9 collective-permute-start
  10.4 15.1 %collective-permute-start.1 = (f32[8,8,2048]{2,1,0:T(8,128)S(1)}, f32[8,8,2048]{2,1,0:T(8,128)S(1)}, u32[]{:S(2)}, u32[]{:S(2)}) collective-permute-start(f32[8,8,2048]{2,1,0:T(8,128)S(1)} %maximum_select_fusion.5), channel_id=1, source_target_pairs={{0,8},{4,12},{8,0},{12,4},{16,24},{20,28},{24,16},{28,20},{1,9},{5... | collective-permute-start | bytes 1572872 | tf_op jit(solution)/shard_map/ppermute | solution.py:17
  25.6 24.7 %collective-permute-start.2 = (f32[8,16,2048]{2,1,0:T(8,128)S(1)}, f32[8,16,2048]{2,1,0:T(8,128)S(1)}, u32[]{:S(2)}, u32[]{:S(2)}) collective-permute-start(f32[8,16,2048]{2,1,0:T(8,128)S(1)} %maximum_select_fusion.4), channel_id=1, source_target_pairs={{0,16},{4,20},{8,24},{12,28},{16,0},{20,4},{24,8},{28,12},{1,17},{... | collective-permute-start | bytes 3145736 | tf_op jit(solution)/shard_map/ppermute | solution.py:17
Sparse Core Ops, SparseCore 0:
  115.8 20.6 reduce-scatter.1
